TPU v7x, 128 devices: a whole 4x4x4 slice. The times are simulated.
128 devices in a mesh: dp: 16 (over z, x_hi, core), mp: 8 (over x_lo, y).
Axes of the slice: x: 4 (x_hi: 2, x_lo: 2; x = x_hi * 2 + x_lo), y: 4, z: 4, core: 2. Of those that a mesh axis runs over, the one named last changes fastest.
Arguments:
- patches: bfloat16 [512, 256, 1280], P(('dp', 'mp')), may hold values from -6 to 6
- position: bfloat16 [256, 1280], replicated, may hold values from -3 to 3
- keep: int32 [512, 64], P(('dp', 'mp')), may hold values from 0 to 255, as said below
- counts: int32 [512], replicated, may hold values from 1 to 64, as said below
- offsets: int32 [512], replicated, may hold values from 0 to 20479, as said below
- ln_gain: float32 [1, 2, 1280], replicated, may hold values from 0.25 to 1.75
- ln_bias: float32 [1, 2, 1280], replicated, may hold values from -2 to 2
- w_qkv: bfloat16 [1, 3, 1280, 1280], P(None, None, 'dp', 'mp')
- b_qkv: float32 [1, 3, 1280], P(None, None, 'mp'), may hold values from -3 to 3
- w_o: bfloat16 [1, 1280, 1280], P(None, 'mp', 'dp'), may hold values from -0.15625 to 0.15625
- b_o: float32 [1, 1280], replicated, may hold values from -1.5 to 1.5
- w_up: bfloat16 [1, 1280, 5120], P(None, 'dp', 'mp'), may hold values from -0.15625 to 0.15625
- b_up: float32 [1, 5120], P(None, 'mp'), may hold values from -3 to 3
- w_down: bfloat16 [1, 5120, 1280], P(None, 'mp', 'dp'), may hold values from -0.078125 to 0.078125
- b_down: float32 [1, 1280], replicated, may hold values from -1.5 to 1.5
Outputs:
- encoded: bfloat16 [20480, 1280], P(('dp', 'mp'))
Inputs may be any that keep to these rules, and one draw needn't show every extreme that they name: `keep`: the first counts[i] entries of row i are distinct and name image i's visible patches; later entries are unused. `counts`: some image has exactly 64 visible patches. Image i, held by dp index s = i // 32, occupies packed rows offsets[i] to offsets[i] + counts[i] - 1, all inside the aligned block of 80 rows numbered d * 16 + s for some shard d; no two images share a row.
All inputs are finite; a program needn't handle non-finite values.
Results may differ from a plain program's by a relative error of at most 0.015.
Values may be sent and summed in bfloat16 or wider, within the bound.
A program may use at most 64 MiB of HBM per device.

v0:
```python
import math

import jax
import jax.numpy as jnp
from jax import lax
from jax.sharding import PartitionSpec as P

HEAD = 80


def from_everyone(x, axis):
    copies = jnp.broadcast_to(x, (lax.axis_size(axis), *x.shape))
    return lax.all_to_all(copies, axis, split_axis=0, concat_axis=0, tiled=True)


def joined_along(parts, dim):
    parts = jnp.moveaxis(parts, 0, dim)
    lengths = parts.shape
    return parts.reshape(*lengths[:dim], lengths[dim] * lengths[dim + 1], *lengths[dim + 2 :])


def gather_directly(x, axis, dim):
    parts = from_everyone(x, axis)
    return joined_along(parts, dim)


def in_blocks(x, dim, peers):
    lengths = x.shape
    parts = x.reshape(*lengths[:dim], peers, lengths[dim] // peers, *lengths[dim + 1 :])
    return jnp.moveaxis(parts, dim, 0)


def sum_at_owner(x, axis, dim):
    parts = in_blocks(x, dim, lax.axis_size(axis))
    arrived = lax.all_to_all(parts, axis, split_axis=0, concat_axis=0, tiled=True)
    return arrived.astype(jnp.float32).sum(axis=0)


def norm_rows(values, gain_row, shift_row):
    row_mean = jnp.mean(values, axis=-1, keepdims=True)
    centred = values - row_mean
    spread = jnp.mean(centred * centred, axis=-1, keepdims=True)
    return (centred * lax.rsqrt(spread + 1e-06) * gain_row + shift_row).astype(jnp.bfloat16)


def gather_rows(normed):
    return lax.all_gather(normed, "mp", axis=0, tiled=True)


def fold_rows(gathered, weight):
    return jnp.einsum(
        "rd,tdc->trc",
        gathered,
        gather_directly(weight, "dp", 1),
        preferred_element_type=jnp.float32,
    )


def project_sum(left, weight):
    partials = jnp.dot(left, gather_directly(weight, "dp", 1), preferred_element_type=jnp.float32)
    return sum_at_owner(partials.astype(jnp.bfloat16), "mp", 0)


def attend(projected, labels, block_rows):
    row_count = projected.shape[1]
    blocks = row_count // block_rows
    head_count = projected.shape[2] // HEAD
    shaped = projected.reshape(3, blocks, block_rows, head_count, HEAD)
    scores = jnp.einsum(
        "bqhe,bkhe->bhqk", shaped[0], shaped[1], preferred_element_type=jnp.float32
    ) * (1.0 / math.sqrt(HEAD))
    labels_block = labels.reshape(blocks, block_rows)
    matches = labels_block[:, None, :, None] == labels_block[:, None, None, :]
    scores = jnp.where(matches, scores, -jnp.inf)
    row_max = jnp.max(scores, axis=-1, keepdims=True)
    weights = jnp.exp(scores - row_max)
    probabilities = (weights / jnp.sum(weights, axis=-1, keepdims=True)).astype(jnp.bfloat16)
    attended = jnp.einsum(
        "bhqk,bkhe->bqhe", probabilities, shaped[2], preferred_element_type=jnp.float32
    )
    return attended.reshape(row_count, head_count * HEAD).astype(jnp.bfloat16)


def group_rows(item_count, unit_rows):
    factor = 1
    while item_count % (factor * 2) == 0 and factor * unit_rows < 512:
        factor = factor * 2
    return factor * unit_rows


def run_layers(
    stream, labels, block_rows, ln_gain, ln_bias, w_qkv, b_qkv, w_o, b_o, w_up, b_up, w_down, b_down
):
    normed = norm_rows(stream.astype(jnp.float32), ln_gain[0, 0], ln_bias[0, 0])
    projected = (fold_rows(gather_rows(normed), w_qkv[0]) + b_qkv[0][:, None, :]).astype(
        jnp.bfloat16
    )
    attended = attend(projected, labels, block_rows)
    residual = stream.astype(jnp.float32) + project_sum(attended, w_o[0]) + b_o[0]
    normed_mlp = norm_rows(residual, ln_gain[0, 1], ln_bias[0, 1])
    up_proj = fold_rows(gather_rows(normed_mlp), w_up[0][None])[0] + b_up[0]
    hidden = jax.nn.gelu(up_proj, approximate=False).astype(jnp.bfloat16)
    stream = (residual + project_sum(hidden, w_down[0]) + b_down[0]).astype(jnp.bfloat16)
    return stream


def per_device(
    patches,
    position,
    keep,
    counts,
    offsets,
    ln_gain,
    ln_bias,
    w_qkv,
    b_qkv,
    w_o,
    b_o,
    w_up,
    b_up,
    w_down,
    b_down,
):
    local_images = patches.shape[0]
    keep_most = keep.shape[1]
    column_count = patches.shape[2]
    shard_count = lax.axis_size("dp")
    group_size = lax.axis_size("mp")
    images_here = local_images * group_size
    per_slot = (images_here + shard_count - 1) // shard_count
    slot_rows = max(keep_most + 16, per_slot * keep_most * 5 // 8)
    pack_rows = slot_rows * shard_count
    local_rows = pack_rows // group_size
    dp_index = lax.axis_index("dp")
    mp_index = lax.axis_index("mp")
    first_image = dp_index * images_here
    group_counts = lax.dynamic_slice_in_dim(counts, first_image, images_here)
    group_offsets = lax.dynamic_slice_in_dim(offsets, first_image, images_here)
    picked = jnp.take_along_axis(patches, keep[:, :, None], axis=1)
    placed = jnp.take(position, keep, axis=0)
    tokens = (picked.astype(jnp.float32) + placed.astype(jnp.float32)).astype(jnp.bfloat16)
    positions_in = jnp.arange(keep_most, dtype=jnp.int32)
    group_live = positions_in[None, :] < group_counts[:, None]
    shard_index = group_offsets // pack_rows
    base_row = (
        shard_index * slot_rows + group_offsets - shard_index * pack_rows - dp_index * slot_rows
    )
    target = jnp.where(group_live, base_row[:, None] + positions_in[None, :], pack_rows).reshape(-1)
    layer_weights = (ln_gain, ln_bias, w_qkv, b_qkv, w_o, b_o, w_up, b_up, w_down, b_down)
    image_ids = jnp.arange(counts.shape[0], dtype=jnp.int32)
    packed_rows = dp_index * pack_rows + jnp.arange(pack_rows, dtype=jnp.int32)
    inside = (packed_rows[:, None] >= offsets[None, :]) & (
        packed_rows[:, None] < (offsets + counts)[None, :]
    )
    labels = jnp.max(jnp.where(inside, image_ids[None, :] + 1, 0), axis=1) - 1
    featured = lax.all_to_all(
        tokens.reshape(-1, column_count), "mp", split_axis=1, concat_axis=0, tiled=True
    )
    buffer_rows = (
        jnp.zeros((pack_rows, featured.shape[1]), jnp.bfloat16)
        .at[target]
        .set(featured, mode="drop")
    )
    stream = lax.all_to_all(
        lax.all_to_all(buffer_rows, "dp", split_axis=0, concat_axis=0, tiled=True),
        "mp",
        split_axis=0,
        concat_axis=1,
        tiled=True,
    )
    stream = run_layers(stream, labels, group_rows(shard_count, slot_rows), *layer_weights)
    own_labels = lax.dynamic_slice_in_dim(labels, mp_index * local_rows, local_rows)
    output = jnp.where(own_labels[:, None] >= 0, stream, jnp.zeros_like(stream))
    return output


def solution(mesh):
    in_specs = (
        P(("dp", "mp"), None, None),
        P(),
        P(("dp", "mp"), None),
        P(),
        P(),
        P(),
        P(),
        P(None, None, "dp", "mp"),
        P(None, None, "mp"),
        P(None, "mp", "dp"),
        P(),
        P(None, "dp", "mp"),
        P(None, "mp"),
        P(None, "mp", "dp"),
        P(),
    )
    out_specs = P(("dp", "mp"), None)
    return jax.shard_map(
        per_device, mesh=mesh, in_specs=in_specs, out_specs=out_specs, check_vma=False
    )
```

profile of v0, /device:TPU:1, one launch (start us, length us, event | category | flops | bytes accessed | tf_op | source)
XLA Modules:
  0.0 380.2 jit_solution(12381919748836157376)
XLA Ops:
  6.5 0.8 compare_select_fusion.1
  7.4 0.7 bitcast_or_fusion
  8.8 2.9 gather_fusion
  11.8 1.1 copy.60
  13.0 3.2 gather_fusion.1
  16.5 2.2 add_convert_fusion.1
  18.7 6.1 %all-to-all-start = ((bf16[256,8,160]{0,2,1:T(8,128)(2,1)}), bf16[256,8,160]{0,2,1:T(8,128)(2,1)S(1)}, u32[]{:S(2)}, u32[]{:S(2)}) async-start(bf16[256,8,160]{0,2,1:T(8,128)(2,1)} %add_convert_fusion.1), calls=%async_computation | async-start | bytes 1310720 | tf_op jit(solution)/shard_map/all_to_all | solution.py:156
  25.1 8.9 %all-to-all-done = bf16[256,8,160]{0,2,1:T(8,128)(2,1)S(1)} async-done(((bf16[256,8,160]{0,2,1:T(8,128)(2,1)}), bf16[256,8,160]{0,2,1:T(8,128)(2,1)S(1)}, u32[]{:S(2)}, u32[]{:S(2)}) %all-to-all-start) | async-done | bytes 655392 | tf_op jit(solution)/shard_map/all_to_all | solution.py:156
  34.5 9.4 %scatter_custom_fusion = bf16[1280,160]{1,0:T(8,128)(2,1)S(1)} fusion(s32[2048]{0:T(1024)S(1)} %bitcast.171, bf16[2048,160]{1,0:T(8,128)(2,1)S(1)} %bitcast.165, bf16[]{:T(256)} %constant.23.clone.1), kind=kCustom, calls=%fused_computation.69 | custom fusion | bytes 409602 | tf_op jit(solution)/shard_map/scatter | solution.py:162
  43.9 23.0 %all_to_all.68 = bf16[16,80,160]{2,1,0:T(8,128)(2,1)} all-to-all(bf16[16,80,160]{2,1,0:T(8,128)(2,1)S(1)} %bitcast.160), channel_id=1, replica_groups=mesh['dp'=16,'mp'=8] {'dp'}, dimensions={0} | all-to-all | bytes 819200 | tf_op jit(solution)/shard_map/all_to_all | solution.py:165
  66.9 3.5 all-to-all-start.2
  70.6 9.9 %all-to-all-done.2 = bf16[8,160,160]{2,1,0:T(8,128)(2,1)S(1)} async-done(((bf16[8,160,160]{2,1,0:T(8,128)(2,1)}), bf16[8,160,160]{2,1,0:T(8,128)(2,1)S(1)}, u32[]{:S(2)}, u32[]{:S(2)}) %all-to-all-start.2) | async-done | bytes 409632 | tf_op jit(solution)/shard_map/all_to_all | solution.py:164
  81.2 0.8 copy.63
  82.5 1.0 add_convert_fusion.4
  83.6 0.9 broadcast_in_dim.102
  84.5 4.9 %all-to-all-start.4 = ((bf16[16,160,80]{2,1,0:T(8,128)(2,1)}), bf16[16,160,80]{2,1,0:T(8,128)(2,1)S(1)}, u32[]{:S(2)}, u32[]{:S(2)}) async-start(bf16[16,160,80]{2,1,0:T(8,128)(2,1)} %broadcast_in_dim.102), calls=%async_computation.4 | async-start | bytes 1310720 | tf_op jit(solution)/shard_map/all_to_all | solution.py:13
  89.6 19.9 %all-to-all-done.4 = bf16[16,160,80]{2,1,0:T(8,128)(2,1)S(1)} async-done(((bf16[16,160,80]{2,1,0:T(8,128)(2,1)}), bf16[16,160,80]{2,1,0:T(8,128)(2,1)S(1)}, u32[]{:S(2)}, u32[]{:S(2)}) %all-to-all-start.4) | async-done | bytes 409632 | tf_op jit(solution)/shard_map/all_to_all | solution.py:13
  109.5 1.6 broadcast_in_dim.99
  111.1 4.6 %all-to-all-start.3 = ((bf16[16,3,80,160]{2,3,1,0:T(8,128)(2,1)}), bf16[16,3,80,160]{2,3,1,0:T(8,128)(2,1)S(1)}, u32[]{:S(2)}, u32[]{:S(2)}) async-start(bf16[16,3,80,160]{2,3,1,0:T(8,128)(2,1)} %broadcast_in_dim.99), calls=%async_computation.3 | async-start | bytes 3932160 | tf_op jit(solution)/shard_map/all_to_all | solution.py:13
  116.4 1.4 broadcast_compare_fusion
  117.8 2.2 copy.71
  120.0 2.5 reshape.222
  122.5 33.0 %all-to-all-done.3 = bf16[16,3,80,160]{2,3,1,0:T(8,128)(2,1)S(1)} async-done(((bf16[16,3,80,160]{2,3,1,0:T(8,128)(2,1)}), bf16[16,3,80,160]{2,3,1,0:T(8,128)(2,1)S(1)}, u32[]{:S(2)}, u32[]{:S(2)}) %all-to-all-start.3) | async-done | bytes 1228832 | tf_op jit(solution)/shard_map/all_to_all | solution.py:13
  155.5 2.1 copy.65
  157.6 3.5 reshape.221
  161.1 3.7 fusion.90
  165.1 1.0 fusion.80
  166.0 1.1 squeeze.21
  167.1 1.1 squeeze.22
  168.3 6.4 %fusion.81 = (f32[2,2,640]{2,1,0:T(2,128)S(1)}, f32[2,2,640,640]{2,3,1,0:T(8,128)}) fusion(pred[2,640,640]{1,2,0:T(8,128)(4,1)} %broadcast_compare_fusion, bf16[2,640,2,80]{1,0,3,2:T(2,128)(2,1)S(1)} %squeeze.22, bf16[2,640,2,80]{1,0,3,2:T(2,128)(2,1)S(1)} %squeeze.21), kind=kOutput, calls=%fused_computation.126 | convolution fusion | flops 268698240 | bytes 8202240 | tf_op jit(solution)/shard_map/sub | solution.py:76
  174.8 3.6 fusion.29
  178.7 2.8 convolution_convert_fusion.1
  181.5 4.6 %all-to-all-start.5 = ((bf16[8,160,1280]{2,1,0:T(8,128)(2,1)}), bf16[8,160,1280]{2,1,0:T(8,128)(2,1)}, u32[]{:S(2)}, u32[]{:S(2)}) async-start(bf16[8,160,1280]{2,1,0:T(8,128)(2,1)} %bitcast.18), calls=%async_computation.5 | async-start | bytes 6553600 | tf_op jit(solution)/shard_map/all_to_all | solution.py:35
  186.5 38.5 %all-to-all-done.5 = bf16[8,160,1280]{2,1,0:T(8,128)(2,1)} async-done(((bf16[8,160,1280]{2,1,0:T(8,128)(2,1)}), bf16[8,160,1280]{2,1,0:T(8,128)(2,1)}, u32[]{:S(2)}, u32[]{:S(2)}) %all-to-all-start.5) | async-done | bytes 3276832 | tf_op jit(solution)/shard_map/all_to_all | solution.py:35
  224.9 2.4 convert_reduce_fusion.1
  227.4 1.8 reduce_sum.69
  229.2 1.9 fusion.32
  231.1 1.8 multiply_reduce_fusion
  232.9 1.0 add_convert_fusion.3
  234.1 45.2 %all_to_all.69 = bf16[16,1,80,640]{3,2,1,0:T(8,128)(2,1)} all-to-all(bf16[16,1,80,640]{3,2,1,0:T(8,128)(2,1)S(1)} %broadcast_in_dim.103), channel_id=1, replica_groups=mesh['dp'=16,'mp'=8] {'dp'}, dimensions={0} | all-to-all | bytes 3276800 | tf_op jit(solution)/shard_map/all_to_all | solution.py:13
  279.3 1.3 broadcast_in_dim.104
  280.6 4.9 %all-to-all-start.7 = ((bf16[16,640,80]{1,2,0:T(8,128)(2,1)}), bf16[16,640,80]{1,2,0:T(8,128)(2,1)}, u32[]{:S(2)}, u32[]{:S(2)}) async-start(bf16[16,640,80]{1,2,0:T(8,128)(2,1)} %broadcast_in_dim.104), calls=%async_computation.7 | async-start | bytes 3276800 | tf_op jit(solution)/shard_map/all_to_all | solution.py:13
  285.5 25.7 %all-to-all-done.7 = bf16[16,640,80]{1,2,0:T(8,128)(2,1)} async-done(((bf16[16,640,80]{1,2,0:T(8,128)(2,1)}), bf16[16,640,80]{1,2,0:T(8,128)(2,1)}, u32[]{:S(2)}, u32[]{:S(2)}) %all-to-all-start.7) | async-done | bytes 1638432 | tf_op jit(solution)/shard_map/all_to_all | solution.py:13
  311.2 15.2 %convolution_convert_fusion = bf16[1280,1280]{1,0:T(8,128)(2,1)} fusion(bf16[640,1280]{0,1:T(8,128)(2,1)} %bitcast.28, bf16[1280,1280]{1,0:T(8,128)(2,1)} %all-gather.5.cloned.1.call-done, bf16[1280,640]{1,0:T(8,128)(2,1)S(1)} %bitcast.162, f32[640]{0:T(1024)S(1)} %reduce.11), kind=kOutput, calls=%fused_computation.4 | convolution fusion | flops 4250009600 | bytes 9832960 | tf_op jit(solution)/shard_map/dot_general | solution.py:60
  326.4 4.6 %all-to-all-start.8 = ((bf16[8,160,1280]{2,1,0:T(8,128)(2,1)}), bf16[8,160,1280]{2,1,0:T(8,128)(2,1)}, u32[]{:S(2)}, u32[]{:S(2)}) async-start(bf16[8,160,1280]{2,1,0:T(8,128)(2,1)} %bitcast.154), calls=%async_computation.8 | async-start | bytes 6553600 | tf_op jit(solution)/shard_map/all_to_all | solution.py:35
  331.2 38.7 %all-to-all-done.8 = bf16[8,160,1280]{2,1,0:T(8,128)(2,1)} async-done(((bf16[8,160,1280]{2,1,0:T(8,128)(2,1)}), bf16[8,160,1280]{2,1,0:T(8,128)(2,1)}, u32[]{:S(2)}, u32[]{:S(2)}) %all-to-all-start.8) | async-done | bytes 3276832 | tf_op jit(solution)/shard_map/all_to_all | solution.py:35
  369.9 2.5 convert_reduce_fusion
  372.4 1.0 fusion.33
  (83 shorter events, 5.6 us)
Async XLA Ops:
  6.5 6.4 %copy-start = (bf16[4,256,1280]{2,1,0:T(8,128)(2,1)S(1)}, bf16[4,256,1280]{2,1,0:T(8,128)(2,1)}, u32[]{:S(2)}) copy-start(bf16[4,256,1280]{2,1,0:T(8,128)(2,1)} %param.15) | copy-start | bytes 7864324
  16.2 8.6 %copy-start.18 = (s32[512]{0:T(512)S(1)}, s32[512]{0:T(512)}, u32[]{:S(2)}) copy-start(s32[512]{0:T(512)} %param.18) | copy-start | bytes 6148
  16.2 8.7 %copy-start.11 = (s32[512]{0:T(512)S(1)}, s32[512]{0:T(512)}, u32[]{:S(2)}) copy-start(s32[512]{0:T(512)} %param.19) | copy-start | bytes 6148
  18.7 51.8 %copy-start.12 = (f32[1,2,1280]{2,1,0:T(2,128)S(1)}, f32[1,2,1280]{2,1,0:T(2,128)}, u32[]{:S(2)}) copy-start(f32[1,2,1280]{2,1,0:T(2,128)} %param.21) | copy-start | bytes 30724
  18.7 51.8 %copy-start.13 = (f32[1,2,1280]{2,1,0:T(2,128)S(1)}, f32[1,2,1280]{2,1,0:T(2,128)}, u32[]{:S(2)}) copy-start(f32[1,2,1280]{2,1,0:T(2,128)} %param.20) | copy-start | bytes 30724
  18.7 15.3 %all-to-all-start = ((bf16[256,8,160]{0,2,1:T(8,128)(2,1)}), bf16[256,8,160]{0,2,1:T(8,128)(2,1)S(1)}, u32[]{:S(2)}, u32[]{:S(2)}) async-start(bf16[256,8,160]{0,2,1:T(8,128)(2,1)} %add_convert_fusion.1), calls=%async_computation | async-start | bytes 1310720 | tf_op jit(solution)/shard_map/all_to_all | solution.py:156
  66.9 13.5 %all-to-all-start.2 = ((bf16[8,160,160]{2,1,0:T(8,128)(2,1)}), bf16[8,160,160]{2,1,0:T(8,128)(2,1)S(1)}, u32[]{:S(2)}, u32[]{:S(2)}) async-start(bf16[8,160,160]{2,1,0:T(8,128)(2,1)} %bitcast.7), calls=%async_computation.2 | async-start | bytes 1310720 | tf_op jit(solution)/shard_map/all_to_all | solution.py:164
  70.5 90.7 %all-gather.3.cloned.1.call-start = ((), (), s32[]{:S(2)}) async-start(), calls=%async_computation.9 | async-start | bytes 3686400 | tf_op jit(solution)/shard_map/all_gather | solution.py:47
  81.1 2.4 copy-start.10
  81.9 7.5 %copy-start.7 = (bf16[1,3,80,160]{3,2,1,0:T(8,128)(2,1)S(1)}, bf16[1,3,80,160]{3,2,1,0:T(8,128)(2,1)}, u32[]{:S(2)}) copy-start(bf16[1,3,80,160]{3,2,1,0:T(8,128)(2,1)} %param.22) | copy-start | bytes 230404
  84.5 25.0 %all-to-all-start.4 = ((bf16[16,160,80]{2,1,0:T(8,128)(2,1)}), bf16[16,160,80]{2,1,0:T(8,128)(2,1)S(1)}, u32[]{:S(2)}, u32[]{:S(2)}) async-start(bf16[16,160,80]{2,1,0:T(8,128)(2,1)} %broadcast_in_dim.102), calls=%async_computation.4 | async-start | bytes 1310720 | tf_op jit(solution)/shard_map/all_to_all | solution.py:13
  89.4 26.3 %copy-start.16 = (f32[1,3,160]{2,0,1:T(1,128)S(1)}, f32[1,3,160]{2,0,1:T(1,128)}, u32[]{:S(2)}) copy-start(f32[1,3,160]{2,0,1:T(1,128)} %param.23) | copy-start | bytes 5764
  109.5 1.6 copy-start.4
  111.1 44.4 %all-to-all-start.3 = ((bf16[16,3,80,160]{2,3,1,0:T(8,128)(2,1)}), bf16[16,3,80,160]{2,3,1,0:T(8,128)(2,1)S(1)}, u32[]{:S(2)}, u32[]{:S(2)}) async-start(bf16[16,3,80,160]{2,3,1,0:T(8,128)(2,1)} %broadcast_in_dim.99), calls=%async_computation.3 | async-start | bytes 3932160 | tf_op jit(solution)/shard_map/all_to_all | solution.py:13
  174.7 4.0 %copy-start.5 = (bf16[160,1280]{1,0:T(8,128)(2,1)S(1)}, bf16[160,1280]{1,0:T(8,128)(2,1)}, u32[]{:S(2)}) copy-start(bf16[160,1280]{1,0:T(8,128)(2,1)} %reshape.222) | copy-start | bytes 1228804
  181.5 4.9 %copy-start.14 = (f32[1,1280]{1,0:T(1,128)S(1)}, f32[1,1280]{1,0:T(1,128)}, u32[]{:S(2)}) copy-start(f32[1,1280]{1,0:T(1,128)} %param.25) | copy-start | bytes 15364
  181.5 43.4 %all-to-all-start.5 = ((bf16[8,160,1280]{2,1,0:T(8,128)(2,1)}), bf16[8,160,1280]{2,1,0:T(8,128)(2,1)}, u32[]{:S(2)}, u32[]{:S(2)}) async-start(bf16[8,160,1280]{2,1,0:T(8,128)(2,1)} %bitcast.18), calls=%async_computation.5 | async-start | bytes 6553600 | tf_op jit(solution)/shard_map/all_to_all | solution.py:35
  186.1 125.1 %all-gather.5.cloned.1.call-start = ((), (), s32[]{:S(2)}) async-start(), calls=%async_computation.10 | async-start | bytes 3686400 | tf_op jit(solution)/shard_map/all_gather | solution.py:47
  227.4 6.5 %copy-start.2 = (f32[160,1280]{1,0:T(8,128)}, f32[160,1280]{1,0:T(8,128)S(1)}, u32[]{:S(2)}) copy-start(f32[160,1280]{1,0:T(8,128)S(1)} %convert_reduce_fusion.1) | copy-start | bytes 2457604
  229.2 4.7 %copy-start.8 = (bf16[1,80,640]{2,1,0:T(8,128)(2,1)S(1)}, bf16[1,80,640]{2,1,0:T(8,128)(2,1)}, u32[]{:S(2)}) copy-start(bf16[1,80,640]{2,1,0:T(8,128)(2,1)} %param.26) | copy-start | bytes 307204
  232.9 46.4 %copy-start.9 = (bf16[1,640,80]{1,2,0:T(8,128)(2,1)S(1)}, bf16[1,640,80]{1,2,0:T(8,128)(2,1)}, u32[]{:S(2)}) copy-start(bf16[1,640,80]{1,2,0:T(8,128)(2,1)} %param.28) | copy-start | bytes 307204
  279.3 6.2 %copy-start.17 = (f32[1,640]{1,0:T(1,128)S(1)}, f32[1,640]{1,0:T(1,128)}, u32[]{:S(2)}) copy-start(f32[1,640]{1,0:T(1,128)} %param.27) | copy-start | bytes 7684
  279.3 32.0 %copy-start.6 = (bf16[16,1,80,640]{3,2,1,0:T(8,128)(2,1)S(1)}, bf16[16,1,80,640]{3,2,1,0:T(8,128)(2,1)}, u32[]{:S(2)}) copy-start(bf16[16,1,80,640]{3,2,1,0:T(8,128)(2,1)} %all_to_all.69) | copy-start | bytes 4915204
  280.6 30.6 %all-to-all-start.7 = ((bf16[16,640,80]{1,2,0:T(8,128)(2,1)}), bf16[16,640,80]{1,2,0:T(8,128)(2,1)}, u32[]{:S(2)}, u32[]{:S(2)}) async-start(bf16[16,640,80]{1,2,0:T(8,128)(2,1)} %broadcast_in_dim.104), calls=%async_computation.7 | async-start | bytes 3276800 | tf_op jit(solution)/shard_map/all_to_all | solution.py:13
  326.4 4.6 %copy-start.15 = (f32[1,1280]{1,0:T(1,128)S(1)}, f32[1,1280]{1,0:T(1,128)}, u32[]{:S(2)}) copy-start(f32[1,1280]{1,0:T(1,128)} %param.29) | copy-start | bytes 15364
  326.4 43.4 %all-to-all-start.8 = ((bf16[8,160,1280]{2,1,0:T(8,128)(2,1)}), bf16[8,160,1280]{2,1,0:T(8,128)(2,1)}, u32[]{:S(2)}, u32[]{:S(2)}) async-start(bf16[8,160,1280]{2,1,0:T(8,128)(2,1)} %bitcast.154), calls=%async_computation.8 | async-start | bytes 6553600 | tf_op jit(solution)/shard_map/all_to_all | solution.py:35
  331.1 42.3 %copy-start.1 = (bf16[4,256,1280]{2,1,0:T(8,128)(2,1)S(1)}, bf16[4,256,1280]{2,1,0:T(8,128)(2,1)}, u32[]{:S(2)}) copy-start(bf16[4,256,1280]{2,1,0:T(8,128)(2,1)} %param.15) | copy-start | bytes 7864324
  369.9 2.5 copy-start.3
Sparse Core Ops, SparseCore 0:
  83.7 58.6 all-gather.2
  234.1 56.5 all-gather.4
where the time goes:
time: 382 us; the launch traced here: 380 us
  waiting for transfers between devices  174 us (46%)
  blocking collectives  68.2 us (18%)
  local copies, waits for them, and re-layouts  39.2 us (10%)
  starting transfers between devices  33.5 us (9%)
  matrix products  31.7 us (8%)
  other arithmetic  19.3 us (5%)
  between operations  13.8 us (4%)
    all_to_all x3, waiting for transfers between devices, from_everyone(): return lax.all_to_all(copies, axis, split_axis=0, concat_axis=0, tiled=True)  78.5 us
    all_to_all x2, waiting for transfers between devices, sum_at_owner(): lax.all_to_all(parts, axis, split_axis=0, concat_axis=0, tiled=True)  77.2 us
    all_to_all x1, blocking collectives, from_everyone(): return lax.all_to_all(copies, axis, split_axis=0, concat_axis=0, tiled=True)  45.2 us
    all_to_all x1, blocking collectives, per_device(): lax.all_to_all(buffer_rows, 'dp', split_axis=0, concat_axis=0, tiled=True)  23 us
    dot_general x2, matrix products, project_sum(): jnp.dot(left, gather_directly(weight, 'dp', 1), preferred_element_type=jn...  18 us
    all_to_all x3, starting transfers between devices, from_everyone(): return lax.all_to_all(copies, axis, split_axis=0, concat_axis=0, tiled=True)  14.4 us
    all_to_all x1, waiting for transfers between devices, per_device(): lax.all_to_all(lax.all_to_all(buffer_rows, 'dp', split_axis=0, concat_axi...  9.86 us
    scatter x1, local copies, waits for them, and re-layouts, per_device(): buffer_rows = jnp.zeros((pack_rows, featured.shape[1]), jnp.bfloat16).at[...  9.41 us
  transfers between devices with their start and end apart: 9, of which 7 were waited for; matrix products, arithmetic and copies ran while one was open for 5% of the time, Pallas kernels for 0%

commit v1 on v0

v1 whole, which is shorter than its diff:
```python
import jax
import jax.numpy as jnp
from jax import lax
from jax.experimental import pallas as pl
from jax.experimental.pallas import tpu as pltpu
from jax.sharding import PartitionSpec as P

BF = jnp.bfloat16
F32 = jnp.float32
MESH = pl.DeviceIdType.MESH
ALL = slice(None)
D = 1280
HEAD = 80
SLOT = 80
ROWS = 160
KEEP = 64
SCALE = 1.0 / HEAD**0.5

ORDERS = ("xyz", "yzx", "zxy")
SECTIONS = (
    ((0, 256), (640, 256), (1280, 128)),
    ((256, 256), (896, 128), (1408, 256)),
    ((512, 128), (1024, 256), (1664, 256)),
)
LANES = 1920
N_SEM = 124


def place():
    dp, mp = lax.axis_index("dp"), lax.axis_index("mp")
    return {
        "x": lax.rem(dp // 2, 2) * 2 + mp // 4,
        "y": lax.rem(mp, 4),
        "z": dp // 4,
        "c": lax.rem(dp, 2),
    }


def device(p):
    return (p["z"] * 4 + (p["x"] // 2) * 2 + p["c"], lax.rem(p["x"], 2) * 4 + p["y"])


def shifted(p, dim, by):
    return {**p, dim: lax.rem(p[dim] + by + 4, 4)}


def other_core(p):
    return {**p, "c": 1 - p["c"]}


def slab(colour, phase, p, half=None):
    free = ORDERS[colour][: phase - 1]
    at = {"xl": lax.rem(p["x"], 2), "xh": p["x"] // 2, "y": p["y"], "z": p["z"], "r": ALL}
    for dim in free:
        for part in ("xl", "xh") if dim == "x" else (dim,):
            at[part] = ALL
    if half is not None:
        if phase == 1:
            at["r"] = pl.ds(0, 48) if half == 0 else pl.ds(48, 32)
        else:
            part, count = ("xl", 1) if free[0] == "x" else (free[0], 2)
            at[part] = pl.ds(half * count, count)
    return (at["xl"], at["y"], at["z"], at["xh"], p["c"], at["r"])


class Transfer:
    def __init__(self, owner, sent, received, lanes, target):
        number = owner.count
        owner.count += 1
        self.owner = owner

        def copy(where):
            ref = owner.ref.at[where + (pl.ds(*lanes),)]
            return pltpu.make_async_remote_copy(
                src_ref=ref,
                dst_ref=ref,
                send_sem=owner.send.at[number],
                recv_sem=owner.recv.at[number],
                device_id=device(target),
                device_id_type=MESH,
            )

        self.out, self.into = copy(sent), copy(received)

    def start(self):
        self.out.start()
        self.owner.started.append(self.out)

    def wait(self):
        self.into.wait_recv()


class Gather:
    def __init__(self, p, ref, send, recv):
        self.p, self.ref, self.send, self.recv = p, ref, send, recv
        self.count, self.started = 0, []
        mate = other_core(p)
        self.own = Transfer(self, slab(0, 1, p), slab(0, 1, mate), (0, LANES), mate)
        self.first = [self.phase(k, 1, (640 * k, 640)) for k in range(3)]
        self.second = [self.phase(k, 2, (640 * k, 640)) for k in range(3)]
        self.third = [[self.phase(k, 3, s[k]) for k in range(3)] for s in SECTIONS]

    def phase(self, k, number, lanes):
        p = self.p
        dim = ORDERS[k][number - 1]
        up, down, far = shifted(p, dim, 1), shifted(p, dim, -1), shifted(p, dim, 2)
        mate = other_core(p)

        def at(q, half=None):
            return slab(k, number, q, half)

        def copy(sent, received, target):
            return Transfer(self, sent, received, lanes, target)

        return {
            "full_up": copy(at(p), at(down), up),
            "full_down": copy(at(p), at(up), down),
            "half_up": copy(at(down, 0), at(far, 0), up),
            "half_down": copy(at(up, 1), at(far, 1), down),
            "mate_down": copy(at(down), at(other_core(down)), mate),
            "mate_up": copy(at(up), at(other_core(up)), mate),
            "mate_far0": copy(at(far, 0), at(other_core(far), 0), mate),
            "mate_far1": copy(at(far, 1), at(other_core(far), 1), mate),
        }

    def fulls(self, group):
        for f in group:
            f["full_up"].start()
            f["full_down"].start()

    def halves(self, group):
        for f in group:
            f["full_up"].wait()
            f["half_up"].start()
            f["full_down"].wait()
            f["half_down"].start()
        for f in group:
            f["mate_down"].start()
            f["mate_up"].start()

    def far(self, group):
        for f in group:
            f["half_up"].wait()
            f["half_down"].wait()

    def far_to_mate(self, group):
        for f in group:
            f["mate_far0"].start()
            f["mate_far1"].start()

    def from_mate(self, group):
        for f in group:
            for name in ("mate_down", "mate_up", "mate_far0", "mate_far1"):
                f[name].wait()


def norm(values, gain, shift):
    mean = jnp.mean(values, axis=-1, keepdims=True)
    centred = values - mean
    spread = jnp.mean(centred * centred, axis=-1, keepdims=True)
    return (centred * lax.rsqrt(spread + 1e-06) * gain + shift).astype(BF)


def dot(a, b, contract=((1,), (0,))):
    return lax.dot_general(a, b, (contract, ((), ())), preferred_element_type=F32)


NT = ((1,), (1,))
TN = ((0,), (0,))


def kernel(
    patches,
    position,
    keep,
    counts,
    offsets,
    ln_gain,
    ln_bias,
    w_qkv,
    b_qkv,
    w_o,
    b_o,
    w_up,
    b_up,
    w_down,
    b_down,
    out,
    w,
    pictures,
    places,
    tokens,
    arrived,
    chosen,
    spread,
    stream,
    normed,
    residual,
    hidden,
    biases,
    send,
    recv,
    load,
    send1,
    recv1,
    send1e,
    recv1e,
    sendb,
    recvb,
    send2,
    recv2,
    send2e,
):
    dp, mp = lax.axis_index("dp"), lax.axis_index("mp")
    p = place()
    mate = other_core(p)
    half = lax.rem(dp, 2)
    tail_owner = (lax.rem(dp, 8), lax.rem(dp + 4, 8))
    has_tail = (mp == tail_owner[0]) | (mp == tail_owner[1])
    tail_tile = jnp.where(mp == tail_owner[0], 8, 9)
    goes_home = mp == dp // 2

    arrived[:, :, 128:256] = jnp.zeros((8, 256, 128), BF)

    barrier = pltpu.get_barrier_semaphore()

    def greet(target):
        pl.semaphore_signal(barrier, inc=1, device_id=target, device_id_type=MESH)

    for q in [shifted(p, d, s) for d in "xyz" for s in (1, -1)] + [mate]:
        greet(device(q))
    for k in range(1, 8):
        greet((dp, lax.rem(mp + k, 8)))
    for k in range(2):
        for m in range(8):
            source = mp * 2 + k

            @pl.when(jnp.logical_not((source == dp) & (mp == m)))
            def _():
                greet((source, jnp.int32(m)))

    load_pictures = pltpu.make_async_copy(patches, pictures, load.at[0])
    load_places = pltpu.make_async_copy(position, places, load.at[1])
    load_pictures.start()
    load_places.start()

    xl, xh = lax.rem(p["x"], 2), p["x"] // 2
    mine = (xl, p["y"], p["z"], xh, p["c"], ALL)

    def put(lane, value):
        w[mine + (pl.ds(lane, value.shape[1]),)] = value.astype(BF)

    eye = (
        lax.broadcasted_iota(jnp.int32, (SLOT, SLOT), 0)
        == lax.broadcasted_iota(jnp.int32, (SLOT, SLOT), 1)
    ).astype(F32).astype(BF)
    out_t = dot(eye, w_o[0], NT)
    down_t = dot(eye, w_down[0], NT)
    qkv = [w_qkv[0, t].astype(F32) for t in range(3)]
    put(0, qkv[0][:, :128])
    put(128, qkv[1][:, :128])
    put(640, qkv[2][:, :128])
    put(768, jnp.concatenate([v[:, 128:160] for v in qkv] + [out_t[:, 128:160]], axis=1))
    put(1280, out_t[:, :128])
    put(256, w_up[0, :, 0:256])
    put(896, w_up[0, :, 256:384])
    put(1408, w_up[0, :, 384:640])
    put(512, down_t[:, 0:128])
    put(1024, down_t[:, 128:384])
    put(1664, down_t[:, 384:640])

    for t in range(3):
        biases[mp, t : t + 1, :] = b_qkv[0, t : t + 1, 0:128]
    biases[mp, 3:4, :] = jnp.concatenate(
        [b_qkv[0, t : t + 1, 128:160] for t in range(3)] + [jnp.zeros((1, 32), F32)], axis=1
    )
    for t in range(5):
        biases[mp, 4 + t : 5 + t, :] = b_up[0:1, t * 128 : (t + 1) * 128]

    load_pictures.wait()
    load_places.wait()
    for i in range(4):
        hit = lax.broadcasted_iota(jnp.int32, (256, KEEP), 0) == keep[i : i + 1, :]
        hit = hit.astype(F32).astype(BF)
        picked = dot(hit, pictures[i], TN) + dot(hit, places[...], TN)
        tokens[i * KEEP : (i + 1) * KEEP, :] = picked.astype(BF)

    pl.semaphore_wait(barrier, 30 - goes_home.astype(jnp.int32))

    g = Gather(p, w, send, recv)
    g.fulls(g.first)
    g.own.start()

    def tile(k):
        return pl.ds(pl.multiple_of(k * 128, 128), 128)

    first_sends = []
    for k in range(1, 8):
        peer = lax.rem(mp + k, 8)
        for src, dst, s, r in (
            (tokens.at[:, tile(peer)], arrived.at[mp, :, pl.ds(0, 128)], send1, recv1),
            (biases.at[mp], biases.at[mp], sendb, recvb),
        ):
            copy = pltpu.make_async_remote_copy(
                src_ref=src,
                dst_ref=dst,
                send_sem=s.at[k],
                recv_sem=r.at[mp],
                device_id=(dp, peer),
                device_id_type=MESH,
            )
            copy.start()
            first_sends.append(copy)
    tail_sends = []
    for k in range(2):
        copy = pltpu.make_async_remote_copy(
            src_ref=tokens.at[:, pl.ds(1024 + 128 * k, 128)],
            dst_ref=arrived.at[mp, :, pl.ds(128, 128)],
            send_sem=send1e.at[k],
            recv_sem=recv1e.at[mp],
            device_id=(dp, tail_owner[k]),
            device_id_type=MESH,
        )
        tail_sends.append(copy)

        @pl.when(mp != tail_owner[k])
        def _():
            copy.start()

        @pl.when(mp == tail_owner[k])
        def _():
            arrived[mp, :, 128:256] = tokens[:, 1024 + 128 * k : 1152 + 128 * k]

    arrived[mp, :, 0:128] = tokens[:, tile(mp)]

    lane = lax.broadcasted_iota(jnp.int32, (16, 128), 1)
    inner = jnp.where(lane < KEEP, lane, lane - KEEP)
    pieces = []
    for k in range(16):
        a, b = dp * 32 + 2 * k, dp * 32 + 2 * k + 1
        count = jnp.where(lane < KEEP, counts[a], counts[b])
        start = jnp.where(lane < KEEP, offsets[a], offsets[b])
        pieces.append(jnp.where(inner < count, start + inner, -1))
    goal = jnp.concatenate(pieces, axis=1)
    sub = lax.broadcasted_iota(jnp.int32, (16, 2048), 0)

    def choose(i, carry):
        shard = i // 5
        row = shard * 1280 + dp * SLOT + (i - shard * 5) * 16
        hit = (goal - row) == sub
        chosen[pl.ds(pl.multiple_of(i * 16, 16), 16), :] = hit.astype(F32).astype(BF)
        return carry

    lax.fori_loop(0, 40, choose, 0)
    g.halves(g.first)
    lax.fori_loop(40, 80, choose, 0)

    labels_row, labels_col = [], []
    for h in range(2):
        first = dp * 1280 + (mp * 2 + h) * SLOT
        down = first + lax.broadcasted_iota(jnp.int32, (SLOT, 128), 0)
        across = first + lax.broadcasted_iota(jnp.int32, (SLOT, 128), 1)

        def mark(i, carry):
            image = (mp * 2 + h) * 32 + i
            low = offsets[image]
            high = low + counts[image]
            return tuple(
                jnp.where((rows >= low) & (rows < high), i + 1, old)
                for rows, old in zip((down, across), carry)
            )

        zero = jnp.zeros((SLOT, 128), jnp.int32)
        col, row = lax.fori_loop(0, 32, mark, (zero, zero))
        labels_col.append(col)
        labels_row.append(row)
    same = [(labels_col[h] == labels_row[h])[:, :SLOT] for h in range(2)]
    used = jnp.concatenate([labels_col[h][:, 0:1] for h in range(2)], axis=0) > 0

    g.far(g.first)
    g.fulls(g.second)
    g.far_to_mate(g.first)

    def wait_first(ref, sem, source):
        pltpu.make_async_remote_copy(
            src_ref=ref,
            dst_ref=ref,
            send_sem=send1.at[0],
            recv_sem=sem.at[source],
            device_id=(dp, source),
            device_id_type=MESH,
        ).wait_recv()

    for k in range(1, 8):
        source = lax.rem(mp + k, 8)
        wait_first(arrived.at[source, :, pl.ds(0, 128)], recv1, source)

    @pl.when(has_tail)
    def _():
        for k in range(1, 8):
            source = lax.rem(mp + k, 8)
            wait_first(arrived.at[source, :, pl.ds(128, 128)], recv1e, source)

    group = arrived[...].reshape(2048, 256)
    for k in range(4):
        rows = pl.ds(k * 320, 320)
        spread[rows, :] = dot(chosen[rows, :], group).astype(BF)

    g.halves(g.second)

    def slot_rows(k):
        return pl.ds(pl.multiple_of(k * SLOT, 16), SLOT)

    second_sends = []
    for k in range(16):
        shard = lax.rem(dp + k, 16)
        for extra in range(2):
            where = tail_tile if extra else mp
            copy = pltpu.make_async_remote_copy(
                src_ref=spread.at[slot_rows(shard), pl.ds(128 * extra, 128)],
                dst_ref=stream.at[slot_rows(half), tile(where)],
                send_sem=(send2e if extra else send2).at[k],
                recv_sem=recv2.at[half, where],
                device_id=(shard, dp // 2),
                device_id_type=MESH,
            )
            away = jnp.logical_not(goes_home) if k == 0 else None
            if extra:
                away = has_tail if away is None else has_tail & away
            if away is None:
                copy.start()
            else:
                pl.when(away)(copy.start)
            second_sends.append((copy, away))

    @pl.when(goes_home)
    def _():
        stream[slot_rows(half), tile(mp)] = spread[slot_rows(dp), 0:128]

    @pl.when(goes_home & has_tail)
    def _():
        stream[slot_rows(half), tile(tail_tile)] = spread[slot_rows(dp), 128:256]

    g.far(g.second)
    g.fulls(g.third[0])
    g.fulls(g.third[1])
    g.far_to_mate(g.second)

    for h in range(2):
        source = mp * 2 + h
        for t in range(10):
            owner = t if t < 8 else lax.rem(source + (t - 8) * 4, 8)

            @pl.when(jnp.logical_not((source == dp) & (mp == owner)))
            def _():
                ref = stream.at[pl.ds(h * SLOT, SLOT), pl.ds(t * 128, 128)]
                pltpu.make_async_remote_copy(
                    src_ref=ref,
                    dst_ref=ref,
                    send_sem=send1.at[0],
                    recv_sem=recv2.at[h, t],
                    device_id=(dp, mp),
                    device_id_type=MESH,
                ).wait_recv()

    for k in range(1, 8):
        source = lax.rem(mp + k, 8)
        wait_first(biases.at[source], recvb, source)

    rows_in = stream[...].astype(F32)
    normed[...] = norm(rows_in, ln_gain[0, 0:1, :], ln_bias[0, 0:1, :])
    residual[...] = rows_in + b_o[...]

    g.halves(g.third[0])
    g.fulls(g.third[2])
    g.halves(g.third[1])
    g.far(g.third[0])
    g.far_to_mate(g.third[0])
    g.own.wait()
    g.from_mate(g.first)
    g.from_mate(g.second)
    g.from_mate(g.third[0])

    def weights(m, *lanes):
        parts = [w[m // 4, lax.rem(m, 4), :, :, :, :, pl.ds(*v)].reshape(D, v[1]) for v in lanes]
        return parts[0] if len(parts) == 1 else jnp.concatenate(parts, axis=1)

    def attention(m, carry):
        rows = normed[...]
        bias = biases[m]

        def projected(lanes, t):
            both = dot(rows, weights(m, lanes))
            return [both[:, 128 * i : 128 * (i + 1)] + bias[t + i : t + i + 1, :] for i in range(2)]

        q, k = projected((0, 256), 0)
        v, tail = projected((640, 256), 2)
        heads = []
        for i, value in enumerate((q, k, v)):
            second = jnp.concatenate([value[:, 80:128], tail[:, 32 * i : 32 * i + 32]], axis=1)
            heads.append((value[:, :80].astype(BF), second.astype(BF)))
        mixed = []
        for n in range(2):
            blocks = []
            for h in range(2):
                part = slice(h * SLOT, (h + 1) * SLOT)
                scores = dot(heads[0][n][part], heads[1][n][part], NT) * SCALE
                scores = jnp.where(same[h], scores, -jnp.inf)
                raised = jnp.exp(scores - jnp.max(scores, axis=-1, keepdims=True))
                share = (raised / jnp.sum(raised, axis=-1, keepdims=True)).astype(BF)
                blocks.append(dot(share, heads[2][n][part]))
            mixed.append(jnp.concatenate(blocks, axis=0))
        left = jnp.concatenate([mixed[0], mixed[1][:, :48]], axis=1).astype(BF)
        right = jnp.concatenate([jnp.zeros((ROWS, 96), F32), mixed[1][:, 48:]], axis=1).astype(BF)
        both = jnp.concatenate([left, right], axis=1)
        residual[...] += dot(both, weights(m, (1280, 128), (768, 128)), NT)
        return carry

    lax.fori_loop(0, 8, attention, 0)
    normed[...] = norm(residual[...], ln_gain[0, 1:2, :], ln_bias[0, 1:2, :])
    residual[...] += b_down[...]

    g.halves(g.third[2])
    g.far(g.third[1])
    g.far_to_mate(g.third[1])
    g.from_mate(g.third[1])

    def up(m, carry):
        rows = normed[...]
        bias = biases[m]
        for lanes, first in (((256, 256), 0), ((896, 128), 2), ((1408, 256), 3)):
            value = dot(rows, weights(m, lanes))
            row = jnp.concatenate(
                [bias[4 + first + i : 5 + first + i, :] for i in range(lanes[1] // 128)], axis=1
            )
            value = value + row
            value = 0.5 * value * (1.0 + lax.erf(value * (0.5**0.5)))
            hidden[m, :, first * 128 : first * 128 + lanes[1]] = value.astype(BF)
        return carry

    lax.fori_loop(0, 8, up, 0)

    g.far(g.third[2])
    g.far_to_mate(g.third[2])
    g.from_mate(g.third[2])

    def down(m, carry):
        residual[...] += dot(
            hidden[m], weights(m, (512, 128), (1024, 256), (1664, 256)), NT
        )
        return carry

    lax.fori_loop(0, 8, down, 0)
    out[...] = jnp.where(used, residual[...], 0.0).astype(BF)

    for copy in g.started + first_sends:
        copy.wait_send()
    for k in range(2):
        pl.when(mp != tail_owner[k])(tail_sends[k].wait_send)
    for copy, away in second_sends:
        if away is None:
            copy.wait_send()
        else:
            pl.when(away)(copy.wait_send)


def per_device(*args):
    vmem = pl.BlockSpec(memory_space=pltpu.VMEM)
    smem = pl.BlockSpec(memory_space=pltpu.SMEM)
    anywhere = pl.BlockSpec(memory_space=pl.ANY)
    specs = [anywhere, anywhere, vmem, smem, smem] + [vmem] * 10
    dma = pltpu.SemaphoreType.DMA
    return pl.pallas_call(
        kernel,
        out_shape=jax.ShapeDtypeStruct((ROWS, D), BF),
        in_specs=specs,
        out_specs=vmem,
        scratch_shapes=[
            pltpu.VMEM((2, 4, 4, 2, 2, SLOT, LANES), BF),
            pltpu.VMEM((4, 256, D), BF),
            pltpu.VMEM((256, D), BF),
            pltpu.VMEM((256, D), BF),
            pltpu.VMEM((8, 256, 256), BF),
            pltpu.VMEM((1280, 2048), BF),
            pltpu.VMEM((1280, 256), BF),
            pltpu.VMEM((ROWS, D), BF),
            pltpu.VMEM((ROWS, D), BF),
            pltpu.VMEM((ROWS, D), F32),
            pltpu.VMEM((8, ROWS, 640), BF),
            pltpu.VMEM((8, 16, 128), F32),
            dma((N_SEM,)),
            dma((N_SEM,)),
            dma((2,)),
            dma((8,)),
            dma((8,)),
            dma((2,)),
            dma((8,)),
            dma((8,)),
            dma((8,)),
            dma((16,)),
            dma((2, 10)),
            dma((16,)),
        ],
        compiler_params=pltpu.CompilerParams(
            collective_id=0, has_side_effects=True, vmem_limit_bytes=62 * 1024 * 1024
        ),
        name="layer",
    )(*args)


def solution(mesh):
    in_specs = (
        P(("dp", "mp"), None, None),
        P(),
        P(("dp", "mp"), None),
        P(),
        P(),
        P(),
        P(),
        P(None, None, "dp", "mp"),
        P(None, None, "mp"),
        P(None, "mp", "dp"),
        P(),
        P(None, "dp", "mp"),
        P(None, "mp"),
        P(None, "mp", "dp"),
        P(),
    )
    return jax.shard_map(
        per_device,
        mesh=mesh,
        in_specs=in_specs,
        out_specs=P(("dp", "mp"), None),
        check_vma=False,
    )
```

time: 382 us -> 142 us (0.37)
  the two profiles are of different devices: /device:TPU:1 before, /device:TPU:41 now
where the time goes in v1:
time: 142 us; the launch traced here: 141 us
  Pallas kernels  137 us (96%)
  local copies, waits for them, and re-layouts  4.75 us (3%)
    pallas_call x1, Pallas kernels, per_device(): pl.pallas_call(kernel, out_shape=jax.ShapeDtypeStruct((ROWS, D), BF), in_...  137 us
    unnamed x3, local copies, waits for them, and re-layouts  4.75 us

profile of v1, /device:TPU:41, one launch (start us, length us, event | category | flops | bytes accessed | tf_op | source)
XLA Modules:
  0.0 141.3 jit_solution(11823424760487592422)
XLA Ops:
  0.0 1.3 copy.16.b_qkv
  1.3 1.7 %copy.17.w_down = bf16[1,640,80]{2,1,0:T(8,128)(2,1)} copy(bf16[1,640,80]{1,2,0:T(8,128)(2,1)} %param.28) | data formatting | bytes 204800 | tf_op args[13]
  3.0 136.6 %layer.1 = bf16[160,1280]{1,0:T(8,128)(2,1)} custom-call(bf16[4,256,1280]{2,1,0:T(8,128)(2,1)} %patches.1, bf16[256,1280]{1,0:T(8,128)(2,1)} %position.1, s32[4,64]{1,0:T(4,128)} %keep.1, s32[512]{0:T(512)} %counts.1, s32[512]{0:T(512)} %offsets.1, f32[1,2,1280]{2,1,0:T(2,128)} %ln_gain.1, f32[1,2,1280]{2,1,0:T(2,128)} %ln_bias.1, ...), custom_call_target="tpu_custom_call" | custom-call | tf_op jit(solution)/shard_map/layer/pallas_call | solution.py:573
  139.5 1.8 %copy.19 = bf16[160,1280]{1,0:T(8,128)(2,1)} copy(bf16[160,1280]{1,0:T(8,128)(2,1)} %layer.1) | data formatting | bytes 819200

commit v2 on v1

--- a/solution.py
+++ b/solution.py
@@ -193,6 +193,7 @@
     arrived,
     chosen,
     spread,
+    slots,
     stream,
     normed,
     residual,
@@ -210,15 +211,17 @@
     send2,
     recv2,
     send2e,
+    recv2e,
+    send3,
+    recv3,
+    send3e,
+    recv3e,
 ):
     dp, mp = lax.axis_index("dp"), lax.axis_index("mp")
     p = place()
     mate = other_core(p)
-    half = lax.rem(dp, 2)
     tail_owner = (lax.rem(dp, 8), lax.rem(dp + 4, 8))
     has_tail = (mp == tail_owner[0]) | (mp == tail_owner[1])
-    tail_tile = jnp.where(mp == tail_owner[0], 8, 9)
-    goes_home = mp == dp // 2
 
     arrived[:, :, 128:256] = jnp.zeros((8, 256, 128), BF)
 
@@ -231,13 +234,8 @@
         greet(device(q))
     for k in range(1, 8):
         greet((dp, lax.rem(mp + k, 8)))
-    for k in range(2):
-        for m in range(8):
-            source = mp * 2 + k
-
-            @pl.when(jnp.logical_not((source == dp) & (mp == m)))
-            def _():
-                greet((source, jnp.int32(m)))
+    for k in range(1, 16):
+        greet((lax.rem(dp + k, 16), mp))
 
     load_pictures = pltpu.make_async_copy(patches, pictures, load.at[0])
     load_places = pltpu.make_async_copy(position, places, load.at[1])
@@ -255,7 +253,7 @@
         == lax.broadcasted_iota(jnp.int32, (SLOT, SLOT), 1)
     ).astype(F32).astype(BF)
     out_t = dot(eye, w_o[0], NT)
-    down_t = dot(eye, w_down[0], NT)
+    down_t = w_down[0]
     qkv = [w_qkv[0, t].astype(F32) for t in range(3)]
     put(0, qkv[0][:, :128])
     put(128, qkv[1][:, :128])
@@ -270,12 +268,18 @@
     put(1664, down_t[:, 384:640])
 
     for t in range(3):
-        biases[mp, t : t + 1, :] = b_qkv[0, t : t + 1, 0:128]
+        biases[mp, t : t + 1, :] = b_qkv[t, 0:1, 0:128]
     biases[mp, 3:4, :] = jnp.concatenate(
-        [b_qkv[0, t : t + 1, 128:160] for t in range(3)] + [jnp.zeros((1, 32), F32)], axis=1
+        [b_qkv[t, 0:1, 128:160] for t in range(3)] + [jnp.zeros((1, 32), F32)], axis=1
     )
     for t in range(5):
         biases[mp, 4 + t : 5 + t, :] = b_up[0:1, t * 128 : (t + 1) * 128]
+
+    pl.semaphore_wait(barrier, 29)
+
+    g = Gather(p, w, send, recv)
+    g.fulls(g.first)
+    g.own.start()
 
     load_pictures.wait()
     load_places.wait()
@@ -284,12 +288,6 @@
         hit = hit.astype(F32).astype(BF)
         picked = dot(hit, pictures[i], TN) + dot(hit, places[...], TN)
         tokens[i * KEEP : (i + 1) * KEEP, :] = picked.astype(BF)
-
-    pl.semaphore_wait(barrier, 30 - goes_home.astype(jnp.int32))
-
-    g = Gather(p, w, send, recv)
-    g.fulls(g.first)
-    g.own.start()
 
     def tile(k):
         return pl.ds(pl.multiple_of(k * 128, 128), 128)
@@ -412,67 +410,98 @@
         return pl.ds(pl.multiple_of(k * SLOT, 16), SLOT)
 
     second_sends = []
-    for k in range(16):
+    for k in range(1, 16):
         shard = lax.rem(dp + k, 16)
         for extra in range(2):
-            where = tail_tile if extra else mp
             copy = pltpu.make_async_remote_copy(
                 src_ref=spread.at[slot_rows(shard), pl.ds(128 * extra, 128)],
-                dst_ref=stream.at[slot_rows(half), tile(where)],
+                dst_ref=slots.at[dp, :, pl.ds(128 * extra, 128)],
                 send_sem=(send2e if extra else send2).at[k],
-                recv_sem=recv2.at[half, where],
-                device_id=(shard, dp // 2),
+                recv_sem=(recv2e if extra else recv2).at[dp],
+                device_id=(shard, mp),
                 device_id_type=MESH,
             )
-            away = jnp.logical_not(goes_home) if k == 0 else None
             if extra:
-                away = has_tail if away is None else has_tail & away
-            if away is None:
+                pl.when(has_tail)(copy.start)
+            else:
                 copy.start()
-            else:
-                pl.when(away)(copy.start)
-            second_sends.append((copy, away))
-
-    @pl.when(goes_home)
-    def _():
-        stream[slot_rows(half), tile(mp)] = spread[slot_rows(dp), 0:128]
-
-    @pl.when(goes_home & has_tail)
-    def _():
-        stream[slot_rows(half), tile(tail_tile)] = spread[slot_rows(dp), 128:256]
+            second_sends.append((copy, has_tail if extra else None))
+    slots[dp] = spread[slot_rows(dp), :]
 
     g.far(g.second)
     g.fulls(g.third[0])
     g.fulls(g.third[1])
     g.far_to_mate(g.second)
 
-    for h in range(2):
-        source = mp * 2 + h
-        for t in range(10):
-            owner = t if t < 8 else lax.rem(source + (t - 8) * 4, 8)
-
-            @pl.when(jnp.logical_not((source == dp) & (mp == owner)))
-            def _():
-                ref = stream.at[pl.ds(h * SLOT, SLOT), pl.ds(t * 128, 128)]
-                pltpu.make_async_remote_copy(
-                    src_ref=ref,
-                    dst_ref=ref,
-                    send_sem=send1.at[0],
-                    recv_sem=recv2.at[h, t],
-                    device_id=(dp, mp),
-                    device_id_type=MESH,
-                ).wait_recv()
+    def wait_copy(ref, sem):
+        pltpu.make_async_remote_copy(
+            src_ref=ref,
+            dst_ref=ref,
+            send_sem=send1.at[0],
+            recv_sem=sem,
+            device_id=device(mate),
+            device_id_type=MESH,
+        ).wait_recv()
+
+    for k in range(1, 16):
+        source = lax.rem(dp + k, 16)
+        wait_copy(slots.at[source, :, pl.ds(0, 128)], recv2.at[source])
+    third_sends = []
+    for k in range(1, 8):
+        peer = lax.rem(mp + k, 8)
+        copy = pltpu.make_async_remote_copy(
+            src_ref=slots.at[pl.ds(peer * 2, 2), :, pl.ds(0, 128)],
+            dst_ref=stream.at[:, :, tile(mp)],
+            send_sem=send3.at[k],
+            recv_sem=recv3.at[mp],
+            device_id=(dp, peer),
+            device_id_type=MESH,
+        )
+        copy.start()
+        third_sends.append((copy, None))
+    stream[:, :, tile(mp)] = slots[pl.ds(mp * 2, 2), :, 0:128]
+    for k in range(4):
+        source = lax.rem(mp + 4 * k, 16)
+        place_tail = pl.ds(1024 + 128 * (k % 2), 128)
+
+        @pl.when(source != dp)
+        def _():
+            wait_copy(slots.at[source, :, pl.ds(128, 128)], recv2e.at[source])
+
+        copy = pltpu.make_async_remote_copy(
+            src_ref=slots.at[source, :, pl.ds(128, 128)],
+            dst_ref=stream.at[lax.rem(source, 2), :, place_tail],
+            send_sem=send3e.at[k],
+            recv_sem=recv3e.at[lax.rem(source, 2), k % 2],
+            device_id=(dp, source // 2),
+            device_id_type=MESH,
+        )
+        away = source // 2 != mp
+        pl.when(away)(copy.start)
+        third_sends.append((copy, away))
+
+        @pl.when(jnp.logical_not(away))
+        def _():
+            stream[lax.rem(source, 2), :, place_tail] = slots[source, :, 128:256]
+
+    g.halves(g.third[0])
+    g.fulls(g.third[2])
 
     for k in range(1, 8):
         source = lax.rem(mp + k, 8)
-        wait_first(biases.at[source], recvb, source)
-
-    rows_in = stream[...].astype(F32)
+        wait_copy(stream.at[:, :, tile(source)], recv3.at[source])
+        wait_copy(biases.at[source], recvb.at[source])
+    for h in range(2):
+        for t in range(2):
+
+            @pl.when(lax.rem(mp * 2 + h + 4 * t, 8) != mp)
+            def _():
+                wait_copy(stream.at[h, :, pl.ds(1024 + 128 * t, 128)], recv3e.at[h, t])
+
+    rows_in = stream[...].reshape(ROWS, D).astype(F32)
     normed[...] = norm(rows_in, ln_gain[0, 0:1, :], ln_bias[0, 0:1, :])
     residual[...] = rows_in + b_o[...]
 
-    g.halves(g.third[0])
-    g.fulls(g.third[2])
     g.halves(g.third[1])
     g.far(g.third[0])
     g.far_to_mate(g.third[0])
@@ -557,7 +586,7 @@
         copy.wait_send()
     for k in range(2):
         pl.when(mp != tail_owner[k])(tail_sends[k].wait_send)
-    for copy, away in second_sends:
+    for copy, away in second_sends + third_sends:
         if away is None:
             copy.wait_send()
         else:
@@ -565,6 +594,9 @@
 
 
 def per_device(*args):
+    args = list(args)
+    args[8] = jnp.transpose(args[8], (1, 0, 2))
+    args[13] = jnp.transpose(args[13], (0, 2, 1))
     vmem = pl.BlockSpec(memory_space=pltpu.VMEM)
     smem = pl.BlockSpec(memory_space=pltpu.SMEM)
     anywhere = pl.BlockSpec(memory_space=pl.ANY)
@@ -583,7 +615,8 @@
             pltpu.VMEM((8, 256, 256), BF),
             pltpu.VMEM((1280, 2048), BF),
             pltpu.VMEM((1280, 256), BF),
-            pltpu.VMEM((ROWS, D), BF),
+            pltpu.VMEM((16, SLOT, 256), BF),
+            pltpu.VMEM((2, SLOT, D), BF),
             pltpu.VMEM((ROWS, D), BF),
             pltpu.VMEM((ROWS, D), F32),
             pltpu.VMEM((8, ROWS, 640), BF),
@@ -598,8 +631,13 @@
             dma((8,)),
             dma((8,)),
             dma((16,)),
-            dma((2, 10)),
             dma((16,)),
+            dma((16,)),
+            dma((16,)),
+            dma((8,)),
+            dma((8,)),
+            dma((4,)),
+            dma((2, 2)),
         ],
         compiler_params=pltpu.CompilerParams(
             collective_id=0, has_side_effects=True, vmem_limit_bytes=62 * 1024 * 1024

time: 142 us -> 125 us (0.88)
  the two profiles are of different devices: /device:TPU:41 before, /device:TPU:1 now
where the time goes in v2:
time: 125 us; the launch traced here: 124 us
  Pallas kernels  122 us (98%)
  local copies, waits for them, and re-layouts  1.78 us (1%)
    pallas_call x1, Pallas kernels, per_device(): pl.pallas_call(kernel, out_shape=jax.ShapeDtypeStruct((ROWS, D), BF), in_...  122 us

profile of v2, /device:TPU:1, one launch (start us, length us, event | category | flops | bytes accessed | tf_op | source)
XLA Modules:
  0.0 123.8 jit_solution(1695946702080932490)
XLA Ops:
  0.0 122.0 %layer.1 = bf16[160,1280]{1,0:T(8,128)(2,1)} custom-call(bf16[4,256,1280]{2,1,0:T(8,128)(2,1)} %patches.1, bf16[256,1280]{1,0:T(8,128)(2,1)} %position.1, s32[4,64]{1,0:T(4,128)} %keep.1, s32[512]{0:T(512)} %counts.1, s32[512]{0:T(512)} %offsets.1, f32[1,2,1280]{2,1,0:T(2,128)} %ln_gain.1, f32[1,2,1280]{2,1,0:T(2,128)} %ln_bias.1, ...), custom_call_target="tpu_custom_call" | custom-call | tf_op jit(solution)/shard_map/layer/pallas_call | solution.py:605
  122.0 1.8 %copy.17 = bf16[160,1280]{1,0:T(8,128)(2,1)} copy(bf16[160,1280]{1,0:T(8,128)(2,1)} %layer.1) | data formatting | bytes 819200

commit v3 on v2

--- a/solution.py
+++ b/solution.py
@@ -17,13 +17,17 @@
 SCALE = 1.0 / HEAD**0.5
 
 ORDERS = ("xyz", "yzx", "zxy")
-SECTIONS = (
-    ((0, 256), (640, 256), (1280, 128)),
-    ((256, 256), (896, 128), (1408, 256)),
-    ((512, 128), (1024, 256), (1664, 256)),
-)
-LANES = 1920
-N_SEM = 124
+COLOURS = ((0, 256), (256, 256), (512, 128))
+Q_K, V_TAIL, OUT, TAIL = (0, 256), (256, 256), (512, 128), (384, 128)
+PLANES = ("yz", "zy")
+RING = ((0, 640), (640, 640))
+UP = ((0, 256), (640, 384))
+DOWN = ((256, 384), (1024, 256))
+N_SEM = 116
+N_MLP = 82
+PIECES = (0, -1, 1, 2)
+FORWARD = {1: (0, -1), -1: (1, 2)}
+FORWARD_TWO = {1: (0,), -1: (1,)}
 
 
 def place():
@@ -55,11 +59,7 @@
         for part in ("xl", "xh") if dim == "x" else (dim,):
             at[part] = ALL
     if half is not None:
-        if phase == 1:
-            at["r"] = pl.ds(0, 48) if half == 0 else pl.ds(48, 32)
-        else:
-            part, count = ("xl", 1) if free[0] == "x" else (free[0], 2)
-            at[part] = pl.ds(half * count, count)
+        at["r"] = pl.ds(0, 48) if half == 0 else pl.ds(48, 32)
     return (at["xl"], at["y"], at["z"], at["xh"], p["c"], at["r"])
 
 
@@ -94,20 +94,114 @@
     def __init__(self, p, ref, send, recv):
         self.p, self.ref, self.send, self.recv = p, ref, send, recv
         self.count, self.started = 0, []
+
+    def cross(self, piece, whole, dim, lanes, pieces, forward):
+        p, mate = self.p, other_core(self.p)
+        out = {"forward": forward}
+        for way in (1, -1):
+            target, source, far = shifted(p, dim, way), shifted(p, dim, -way), shifted(p, dim, 2)
+            for r in pieces:
+                out["full", way, r] = Transfer(self, piece(p, r), piece(source, r), lanes, target)
+            for r in forward[way]:
+                out["half", way, r] = Transfer(self, piece(source, r), piece(far, r), lanes, target)
+        for way in (1, -1, 2):
+            q = shifted(p, dim, way)
+            out["mate", way] = Transfer(self, whole(q), whole(other_core(q)), lanes, mate)
+        return out
+
+    def offer(self, group, pieces):
+        for r in pieces:
+            for f in group:
+                for way in (1, -1):
+                    f["full", way, r].start()
+
+    def relay(self, group, pieces):
+        for r in pieces:
+            for f in group:
+                for way in (1, -1):
+                    f["full", way, r].wait()
+                    if r in f["forward"][way]:
+                        f["half", way, r].start()
+
+    def to_mate(self, group):
+        for f in group:
+            for way in (1, -1):
+                f["mate", way].start()
+
+    def last(self, group):
+        for f in group:
+            for way in (1, -1):
+                for r in f["forward"][way]:
+                    f["half", way, r].wait()
+
+    def last_to_mate(self, group):
+        for f in group:
+            f["mate", 2].start()
+
+    def all_from_mate(self, group):
+        for f in group:
+            for way in (1, -1, 2):
+                f["mate", way].wait()
+
+    def fulls(self, group):
+        for f in group:
+            f["full_up"].start()
+            f["full_down"].start()
+
+    def halves(self, group):
+        for f in group:
+            f["full_up"].wait()
+            f["half_up"].start()
+            f["full_down"].wait()
+            f["half_down"].start()
+        for f in group:
+            f["mate_down"].start()
+            f["mate_up"].start()
+
+    def far(self, group):
+        for f in group:
+            f["half_up"].wait()
+            f["half_down"].wait()
+
+    def far_to_mate(self, group):
+        for f in group:
+            f["mate_far0"].start()
+            f["mate_far1"].start()
+
+    def from_mate(self, group):
+        for f in group:
+            for name in ("mate_down", "mate_up", "mate_far0", "mate_far1"):
+                f[name].wait()
+
+
+class Attention(Gather):
+    def __init__(self, p, ref, send, recv):
+        super().__init__(p, ref, send, recv)
         mate = other_core(p)
-        self.own = Transfer(self, slab(0, 1, p), slab(0, 1, mate), (0, LANES), mate)
-        self.first = [self.phase(k, 1, (640 * k, 640)) for k in range(3)]
-        self.second = [self.phase(k, 2, (640 * k, 640)) for k in range(3)]
-        self.third = [[self.phase(k, 3, s[k]) for k in range(3)] for s in SECTIONS]
-
-    def phase(self, k, number, lanes):
+        self.own = Transfer(self, slab(0, 1, p), slab(0, 1, mate), (0, 640), mate)
+        self.first = [self.ring(k, COLOURS[k]) for k in range(3)]
+        self.second = [self.span(k, 2, COLOURS[k]) for k in range(3)]
+        self.third = [self.span(k, 3, COLOURS[k]) for k in range(3)]
+
+    def span(self, k, number, lanes):
+        inner, dim = ORDERS[k][number - 2], ORDERS[k][number - 1]
+        return self.cross(
+            lambda q, r: slab(k, number - 1, shifted(q, inner, r)),
+            lambda q: slab(k, number, q),
+            dim,
+            lanes,
+            PIECES,
+            FORWARD,
+        )
+
+    def ring(self, k, lanes):
         p = self.p
-        dim = ORDERS[k][number - 1]
+        dim = ORDERS[k][0]
         up, down, far = shifted(p, dim, 1), shifted(p, dim, -1), shifted(p, dim, 2)
         mate = other_core(p)
 
         def at(q, half=None):
-            return slab(k, number, q, half)
+            return slab(k, 1, q, half)
 
         def copy(sent, received, target):
             return Transfer(self, sent, received, lanes, target)
@@ -123,35 +217,48 @@
             "mate_far1": copy(at(far, 1), at(other_core(far), 1), mate),
         }
 
-    def fulls(self, group):
-        for f in group:
-            f["full_up"].start()
-            f["full_down"].start()
-
-    def halves(self, group):
-        for f in group:
-            f["full_up"].wait()
-            f["half_up"].start()
-            f["full_down"].wait()
-            f["half_down"].start()
-        for f in group:
-            f["mate_down"].start()
-            f["mate_up"].start()
-
-    def far(self, group):
-        for f in group:
-            f["half_up"].wait()
-            f["half_down"].wait()
-
-    def far_to_mate(self, group):
-        for f in group:
-            f["mate_far0"].start()
-            f["mate_far1"].start()
-
-    def from_mate(self, group):
-        for f in group:
-            for name in ("mate_down", "mate_up", "mate_far0", "mate_far1"):
-                f[name].wait()
+
+class Mlp(Gather):
+    def __init__(self, p, ref, send, recv):
+        super().__init__(p, ref, send, recv)
+        mate, over = other_core(p), shifted(p, "x", 2)
+        whole = (0, 1280)
+        self.own = Transfer(self, self.at(p), self.at(mate), whole, mate)
+        self.over = Transfer(self, self.at(p), self.at(over), whole, over)
+        self.over_mate = Transfer(self, self.at(over), self.at(other_core(over)), whole, mate)
+        self.ring = [
+            self.cross(
+                lambda q, r: self.at(shifted(q, "x", 2 * r)),
+                lambda q: self.at(q, "x"),
+                PLANES[k][0],
+                RING[k],
+                (0, 1),
+                FORWARD_TWO,
+            )
+            for k in range(2)
+        ]
+        self.up = [self.span(k, UP[k]) for k in range(2)]
+        self.down = [self.span(k, DOWN[k]) for k in range(2)]
+
+    def at(self, q, free=""):
+        return (
+            ALL if "y" in free else q["y"],
+            ALL if "z" in free else q["z"],
+            ALL if "x" in free else q["x"] // 2,
+            q["c"],
+            ALL,
+        )
+
+    def span(self, k, lanes):
+        inner, dim = PLANES[k]
+        return self.cross(
+            lambda q, r: self.at(shifted(q, inner, r), "x"),
+            lambda q: self.at(q, "x" + inner),
+            dim,
+            lanes,
+            PIECES,
+            FORWARD,
+        )
 
 
 def norm(values, gain, shift):
@@ -187,6 +294,7 @@
     b_down,
     out,
     w,
+    w_mlp,
     pictures,
     places,
     tokens,
@@ -196,11 +304,18 @@
     slots,
     stream,
     normed,
+    pair_rows,
     residual,
     hidden,
+    partial,
+    returned,
     biases,
     send,
     recv,
+    send_mlp,
+    recv_mlp,
+    send_pair,
+    recv_pair,
     load,
     send1,
     recv1,
@@ -248,24 +363,24 @@
     def put(lane, value):
         w[mine + (pl.ds(lane, value.shape[1]),)] = value.astype(BF)
 
+    def put_mlp(lane, value):
+        w_mlp[mine[1:] + (pl.ds(lane, value.shape[1]),)] = value
+
     eye = (
         lax.broadcasted_iota(jnp.int32, (SLOT, SLOT), 0)
         == lax.broadcasted_iota(jnp.int32, (SLOT, SLOT), 1)
     ).astype(F32).astype(BF)
     out_t = dot(eye, w_o[0], NT)
-    down_t = w_down[0]
     qkv = [w_qkv[0, t].astype(F32) for t in range(3)]
     put(0, qkv[0][:, :128])
     put(128, qkv[1][:, :128])
-    put(640, qkv[2][:, :128])
-    put(768, jnp.concatenate([v[:, 128:160] for v in qkv] + [out_t[:, 128:160]], axis=1))
-    put(1280, out_t[:, :128])
-    put(256, w_up[0, :, 0:256])
-    put(896, w_up[0, :, 256:384])
-    put(1408, w_up[0, :, 384:640])
-    put(512, down_t[:, 0:128])
-    put(1024, down_t[:, 128:384])
-    put(1664, down_t[:, 384:640])
+    put(256, qkv[2][:, :128])
+    put(384, jnp.concatenate([v[:, 128:160] for v in qkv] + [out_t[:, 128:160]], axis=1))
+    put(512, out_t[:, :128])
+    put_mlp(0, w_up[0, :, 0:256])
+    put_mlp(640, w_up[0, :, 256:640])
+    put_mlp(256, w_down[0, :, 0:384])
+    put_mlp(1024, w_down[0, :, 384:640])
 
     for t in range(3):
         biases[mp, t : t + 1, :] = b_qkv[t, 0:1, 0:128]
@@ -277,9 +392,14 @@
 
     pl.semaphore_wait(barrier, 29)
 
-    g = Gather(p, w, send, recv)
+    g = Attention(p, w, send, recv)
+    mlp = Mlp(p, w_mlp, send_mlp, recv_mlp)
     g.fulls(g.first)
+    mlp.over.start()
+    g.offer(g.second, (0,))
+    mlp.offer(mlp.ring, (0,))
     g.own.start()
+    mlp.own.start()
 
     load_pictures.wait()
     load_places.wait()
@@ -351,6 +471,7 @@
 
     lax.fori_loop(0, 40, choose, 0)
     g.halves(g.first)
+    g.offer(g.second, (-1, 1))
     lax.fori_loop(40, 80, choose, 0)
 
     labels_row, labels_col = [], []
@@ -376,8 +497,14 @@
     used = jnp.concatenate([labels_col[h][:, 0:1] for h in range(2)], axis=0) > 0
 
     g.far(g.first)
-    g.fulls(g.second)
+    g.offer(g.second, (2,))
+    g.offer(g.third, (0,))
     g.far_to_mate(g.first)
+
+    g.relay(g.second, (0, -1, 1))
+    mlp.over.wait()
+    mlp.offer(mlp.ring, (1,))
+    mlp.over_mate.start()
 
     def wait_first(ref, sem, source):
         pltpu.make_async_remote_copy(
@@ -403,8 +530,6 @@
     for k in range(4):
         rows = pl.ds(k * 320, 320)
         spread[rows, :] = dot(chosen[rows, :], group).astype(BF)
-
-    g.halves(g.second)
 
     def slot_rows(k):
         return pl.ds(pl.multiple_of(k * SLOT, 16), SLOT)
@@ -428,10 +553,18 @@
             second_sends.append((copy, has_tail if extra else None))
     slots[dp] = spread[slot_rows(dp), :]
 
-    g.far(g.second)
-    g.fulls(g.third[0])
-    g.fulls(g.third[1])
-    g.far_to_mate(g.second)
+    g.relay(g.second, (2,))
+    g.offer(g.third, (-1, 1))
+    g.to_mate(g.second)
+    g.last(g.second)
+    g.offer(g.third, (2,))
+    g.last_to_mate(g.second)
+
+    mlp.relay(mlp.ring, (0, 1))
+    mlp.to_mate(mlp.ring)
+    mlp.offer(mlp.up, (0,))
+    mlp.last(mlp.ring)
+    mlp.last_to_mate(mlp.ring)
 
     def wait_copy(ref, sem):
         pltpu.make_async_remote_copy(
@@ -484,8 +617,11 @@
         def _():
             stream[lax.rem(source, 2), :, place_tail] = slots[source, :, 128:256]
 
-    g.halves(g.third[0])
-    g.fulls(g.third[2])
+    g.relay(g.third, PIECES)
+    g.to_mate(g.third)
+    mlp.offer(mlp.up, (-1, 1, 2))
+
+    mlp.offer(mlp.down, PIECES)
 
     for k in range(1, 8):
         source = lax.rem(mp + k, 8)
@@ -502,13 +638,12 @@
     normed[...] = norm(rows_in, ln_gain[0, 0:1, :], ln_bias[0, 0:1, :])
     residual[...] = rows_in + b_o[...]
 
-    g.halves(g.third[1])
-    g.far(g.third[0])
-    g.far_to_mate(g.third[0])
+    g.last(g.third)
+    g.last_to_mate(g.third)
     g.own.wait()
     g.from_mate(g.first)
-    g.from_mate(g.second)
-    g.from_mate(g.third[0])
+    g.all_from_mate(g.second)
+    g.all_from_mate(g.third)
 
     def weights(m, *lanes):
         parts = [w[m // 4, lax.rem(m, 4), :, :, :, :, pl.ds(*v)].reshape(D, v[1]) for v in lanes]
@@ -522,8 +657,8 @@
             both = dot(rows, weights(m, lanes))
             return [both[:, 128 * i : 128 * (i + 1)] + bias[t + i : t + i + 1, :] for i in range(2)]
 
-        q, k = projected((0, 256), 0)
-        v, tail = projected((640, 256), 2)
+        q, k = projected(Q_K, 0)
+        v, tail = projected(V_TAIL, 2)
         heads = []
         for i, value in enumerate((q, k, v)):
             second = jnp.concatenate([value[:, 80:128], tail[:, 32 * i : 32 * i + 32]], axis=1)
@@ -542,47 +677,97 @@
         left = jnp.concatenate([mixed[0], mixed[1][:, :48]], axis=1).astype(BF)
         right = jnp.concatenate([jnp.zeros((ROWS, 96), F32), mixed[1][:, 48:]], axis=1).astype(BF)
         both = jnp.concatenate([left, right], axis=1)
-        residual[...] += dot(both, weights(m, (1280, 128), (768, 128)), NT)
+        residual[...] += dot(both, weights(m, OUT, TAIL), NT)
         return carry
 
-    lax.fori_loop(0, 8, attention, 0)
-    normed[...] = norm(residual[...], ln_gain[0, 1:2, :], ln_bias[0, 1:2, :])
+    lax.fori_loop(0, 4, attention, 0)
+    mlp.relay(mlp.up, PIECES)
+    mlp.to_mate(mlp.up)
+    lax.fori_loop(4, 8, attention, 0)
+    pair_rows[0:ROWS, :] = norm(residual[...], ln_gain[0, 1:2, :], ln_bias[0, 1:2, :])
     residual[...] += b_down[...]
 
-    g.halves(g.third[2])
-    g.far(g.third[1])
-    g.far_to_mate(g.third[1])
-    g.from_mate(g.third[1])
-
-    def up(m, carry):
-        rows = normed[...]
-        bias = biases[m]
-        for lanes, first in (((256, 256), 0), ((896, 128), 2), ((1408, 256), 3)):
-            value = dot(rows, weights(m, lanes))
-            row = jnp.concatenate(
-                [bias[4 + first + i : 5 + first + i, :] for i in range(lanes[1] // 128)], axis=1
-            )
-            value = value + row
+    sides = (device(shifted(p, "x", 1)), device(shifted(p, "x", -1)))
+    pair_sends = []
+
+    def to_pair(src, dst, number, target):
+        copy = pltpu.make_async_remote_copy(
+            src_ref=src,
+            dst_ref=dst,
+            send_sem=send_pair.at[number],
+            recv_sem=recv_pair.at[number],
+            device_id=target,
+            device_id_type=MESH,
+        )
+        copy.start()
+        pair_sends.append(copy)
+
+    for k in range(2):
+        to_pair(
+            pair_rows.at[pl.ds(SLOT * k, SLOT)],
+            pair_rows.at[pl.ds(ROWS + SLOT * k, SLOT)],
+            k,
+            sides[k],
+        )
+
+    mlp.relay(mlp.down, PIECES)
+    mlp.to_mate(mlp.down)
+    mlp.last(mlp.up)
+    mlp.last_to_mate(mlp.up)
+    mlp.own.wait()
+    mlp.over_mate.wait()
+    mlp.all_from_mate(mlp.ring)
+    mlp.all_from_mate(mlp.up)
+    pair_sends[0].wait_recv()
+    pair_sends[1].wait_recv()
+
+    def up(y, carry):
+        rows = pair_rows[...]
+        bias = biases[xl * 4 + y]
+        first = 0
+        for lanes in UP:
+            value = dot(rows, w_mlp[y, :, :, :, :, pl.ds(*lanes)].reshape(D, lanes[1]))
+            tiles = lanes[1] // 128
+            row = [bias[4 + first + i : 5 + first + i, :] for i in range(tiles)]
+            value = value + jnp.concatenate(row, axis=1)
             value = 0.5 * value * (1.0 + lax.erf(value * (0.5**0.5)))
-            hidden[m, :, first * 128 : first * 128 + lanes[1]] = value.astype(BF)
+            hidden[y, :, first * 128 : (first + tiles) * 128] = value.astype(BF)
+            first += tiles
         return carry
 
-    lax.fori_loop(0, 8, up, 0)
-
-    g.far(g.third[2])
-    g.far_to_mate(g.third[2])
-    g.from_mate(g.third[2])
-
-    def down(m, carry):
-        residual[...] += dot(
-            hidden[m], weights(m, (512, 128), (1024, 256), (1664, 256)), NT
-        )
+    lax.fori_loop(0, 4, up, 0)
+
+    mlp.last(mlp.down)
+    mlp.last_to_mate(mlp.down)
+    mlp.all_from_mate(mlp.down)
+
+    def down_weights(y, z, count):
+        parts = [
+            w_mlp[y, pl.ds(z, count), :, :, :, pl.ds(*v)].reshape(count * 320, v[1]) for v in DOWN
+        ]
+        return jnp.concatenate(parts, axis=1)
+
+    for n in range(2):
+        total = 0.0
+        for y in range(4):
+            total = total + dot(hidden[y, ROWS:, :], down_weights(y, 2 * n, 2), NT)
+        columns = pl.ds(640 * n, 640)
+        partial[:, columns] = total.astype(BF)
+        for k in range(2):
+            block = (pl.ds(SLOT * k, SLOT), columns)
+            to_pair(partial.at[block], returned.at[block], 2 + 2 * n + k, sides[1 - k])
+
+    def down(y, carry):
+        residual[...] += dot(hidden[y, :ROWS, :], down_weights(y, 0, 4), NT)
         return carry
 
-    lax.fori_loop(0, 8, down, 0)
-    out[...] = jnp.where(used, residual[...], 0.0).astype(BF)
-
-    for copy in g.started + first_sends:
+    lax.fori_loop(0, 4, down, 0)
+    for n in range(4):
+        pair_sends[2 + n].wait_recv()
+    total = residual[...] + returned[...].astype(F32)
+    out[...] = jnp.where(used, total, 0.0).astype(BF)
+
+    for copy in g.started + mlp.started + first_sends + pair_sends:
         copy.wait_send()
     for k in range(2):
         pl.when(mp != tail_owner[k])(tail_sends[k].wait_send)
@@ -608,7 +793,8 @@
         in_specs=specs,
         out_specs=vmem,
         scratch_shapes=[
-            pltpu.VMEM((2, 4, 4, 2, 2, SLOT, LANES), BF),
+            pltpu.VMEM((2, 4, 4, 2, 2, SLOT, 640), BF),
+            pltpu.VMEM((4, 4, 2, 2, SLOT, 1280), BF),
             pltpu.VMEM((4, 256, D), BF),
             pltpu.VMEM((256, D), BF),
             pltpu.VMEM((256, D), BF),
@@ -618,11 +804,18 @@
             pltpu.VMEM((16, SLOT, 256), BF),
             pltpu.VMEM((2, SLOT, D), BF),
             pltpu.VMEM((ROWS, D), BF),
+            pltpu.VMEM((2 * ROWS, D), BF),
             pltpu.VMEM((ROWS, D), F32),
-            pltpu.VMEM((8, ROWS, 640), BF),
+            pltpu.VMEM((4, 2 * ROWS, 640), BF),
+            pltpu.VMEM((ROWS, D), BF),
+            pltpu.VMEM((ROWS, D), BF),
             pltpu.VMEM((8, 16, 128), F32),
             dma((N_SEM,)),
             dma((N_SEM,)),
+            dma((N_MLP,)),
+            dma((N_MLP,)),
+            dma((6,)),
+            dma((6,)),
             dma((2,)),
             dma((8,)),
             dma((8,)),

time: 125 us -> 106 us (0.85)
  Pallas kernels: 122 us -> 102 us
    pallas_call x1, Pallas kernels: 122 us -> 102 us  [per_device(): pl.pallas_call(kernel, out_shape=jax.ShapeDtypeStruct((ROWS, D), BF), in_...]
where the time goes in v3:
time: 106 us; the launch traced here: 104 us
  Pallas kernels  102 us (96%)
  local copies, waits for them, and re-layouts  1.78 us (2%)
    pallas_call x1, Pallas kernels, per_device(): pl.pallas_call(kernel, out_shape=jax.ShapeDtypeStruct((ROWS, D), BF), in_...  102 us

profile of v3, /device:TPU:1, one launch (start us, length us, event | category | flops | bytes accessed | tf_op | source)
XLA Modules:
  0.0 104.1 jit_solution(18098946327643658985)
XLA Ops:
  0.0 102.3 %layer.1 = bf16[160,1280]{1,0:T(8,128)(2,1)} custom-call(bf16[4,256,1280]{2,1,0:T(8,128)(2,1)} %patches.1, bf16[256,1280]{1,0:T(8,128)(2,1)} %position.1, s32[4,64]{1,0:T(4,128)} %keep.1, s32[512]{0:T(512)} %counts.1, s32[512]{0:T(512)} %offsets.1, f32[1,2,1280]{2,1,0:T(2,128)} %ln_gain.1, f32[1,2,1280]{2,1,0:T(2,128)} %ln_bias.1, ...), custom_call_target="tpu_custom_call" | custom-call | tf_op jit(solution)/shard_map/layer/pallas_call | solution.py:790
  102.3 1.8 %copy.17 = bf16[160,1280]{1,0:T(8,128)(2,1)} copy(bf16[160,1280]{1,0:T(8,128)(2,1)} %layer.1) | data formatting | bytes 819200

commit v4 on v3

--- a/solution.py
+++ b/solution.py
@@ -16,7 +16,7 @@
 KEEP = 64
 SCALE = 1.0 / HEAD**0.5
 
-ORDERS = ("xyz", "yzx", "zxy")
+ORDERS = ("yxz", "zyx", "xzy")
 COLOURS = ((0, 256), (256, 256), (512, 128))
 Q_K, V_TAIL, OUT, TAIL = (0, 256), (256, 256), (512, 128), (384, 128)
 PLANES = ("yz", "zy")
@@ -469,37 +469,15 @@
         chosen[pl.ds(pl.multiple_of(i * 16, 16), 16), :] = hit.astype(F32).astype(BF)
         return carry
 
-    lax.fori_loop(0, 40, choose, 0)
     g.halves(g.first)
     g.offer(g.second, (-1, 1))
-    lax.fori_loop(40, 80, choose, 0)
-
-    labels_row, labels_col = [], []
-    for h in range(2):
-        first = dp * 1280 + (mp * 2 + h) * SLOT
-        down = first + lax.broadcasted_iota(jnp.int32, (SLOT, 128), 0)
-        across = first + lax.broadcasted_iota(jnp.int32, (SLOT, 128), 1)
-
-        def mark(i, carry):
-            image = (mp * 2 + h) * 32 + i
-            low = offsets[image]
-            high = low + counts[image]
-            return tuple(
-                jnp.where((rows >= low) & (rows < high), i + 1, old)
-                for rows, old in zip((down, across), carry)
-            )
-
-        zero = jnp.zeros((SLOT, 128), jnp.int32)
-        col, row = lax.fori_loop(0, 32, mark, (zero, zero))
-        labels_col.append(col)
-        labels_row.append(row)
-    same = [(labels_col[h] == labels_row[h])[:, :SLOT] for h in range(2)]
-    used = jnp.concatenate([labels_col[h][:, 0:1] for h in range(2)], axis=0) > 0
+    lax.fori_loop(0, 40, choose, 0)
 
     g.far(g.first)
     g.offer(g.second, (2,))
     g.offer(g.third, (0,))
     g.far_to_mate(g.first)
+    lax.fori_loop(40, 80, choose, 0)
 
     g.relay(g.second, (0, -1, 1))
     mlp.over.wait()
@@ -556,13 +534,12 @@
     g.relay(g.second, (2,))
     g.offer(g.third, (-1, 1))
     g.to_mate(g.second)
+    mlp.relay(mlp.ring, (0, 1))
+    mlp.to_mate(mlp.ring)
+    mlp.offer(mlp.up, (0,))
     g.last(g.second)
     g.offer(g.third, (2,))
     g.last_to_mate(g.second)
-
-    mlp.relay(mlp.ring, (0, 1))
-    mlp.to_mate(mlp.ring)
-    mlp.offer(mlp.up, (0,))
     mlp.last(mlp.ring)
     mlp.last_to_mate(mlp.ring)
 
@@ -622,6 +599,29 @@
     mlp.offer(mlp.up, (-1, 1, 2))
 
     mlp.offer(mlp.down, PIECES)
+
+    labels_row, labels_col = [], []
+    for h in range(2):
+        first = dp * 1280 + (mp * 2 + h) * SLOT
+        down = first + lax.broadcasted_iota(jnp.int32, (SLOT, 128), 0)
+        across = first + lax.broadcasted_iota(jnp.int32, (SLOT, 128), 1)
+
+        def mark(i, carry):
+            image = (mp * 2 + h) * 32 + i
+            low = offsets[image]
+            high = low + counts[image]
+            return tuple(
+                jnp.where((rows >= low) & (rows < high), i + 1, old)
+                for rows, old in zip((down, across), carry)
+            )
+
+        zero = jnp.zeros((SLOT, 128), jnp.int32)
+        col, row = lax.fori_loop(0, 32, mark, (zero, zero))
+        labels_col.append(col)
+        labels_row.append(row)
+    same = [(labels_col[h] == labels_row[h])[:, :SLOT] for h in range(2)]
+    used = jnp.concatenate([labels_col[h][:, 0:1] for h in range(2)], axis=0) > 0
+
 
     for k in range(1, 8):
         source = lax.rem(mp + k, 8)

time: 106 us -> 101 us (0.953); the launches traced: 104 us -> 100 us
  Pallas kernels: 102 us -> 98.5 us
    pallas_call x1, Pallas kernels: 102 us -> 98.5 us  [per_device(): pl.pallas_call(kernel, out_shape=jax.ShapeDtypeStruct((ROWS, D), BF), in_...]
where the time goes in v4:
time: 101 us; the launch traced here: 100 us
  Pallas kernels  98.5 us (98%)
  local copies, waits for them, and re-layouts  1.78 us (2%)
    pallas_call x1, Pallas kernels, per_device(): pl.pallas_call(kernel, out_shape=jax.ShapeDtypeStruct((ROWS, D), BF), in_...  98.5 us

profile of v4, /device:TPU:1, one launch (start us, length us, event | category | flops | bytes accessed | tf_op | source)
XLA Modules:
  0.0 100.3 jit_solution(425454041201629206)
XLA Ops:
  0.0 98.5 %layer.1 = bf16[160,1280]{1,0:T(8,128)(2,1)} custom-call(bf16[4,256,1280]{2,1,0:T(8,128)(2,1)} %patches.1, bf16[256,1280]{1,0:T(8,128)(2,1)} %position.1, s32[4,64]{1,0:T(4,128)} %keep.1, s32[512]{0:T(512)} %counts.1, s32[512]{0:T(512)} %offsets.1, f32[1,2,1280]{2,1,0:T(2,128)} %ln_gain.1, f32[1,2,1280]{2,1,0:T(2,128)} %ln_bias.1, ...), custom_call_target="tpu_custom_call" | custom-call | tf_op jit(solution)/shard_map/layer/pallas_call | solution.py:790
  98.5 1.8 %copy.17 = bf16[160,1280]{1,0:T(8,128)(2,1)} copy(bf16[160,1280]{1,0:T(8,128)(2,1)} %layer.1) | data formatting | bytes 819200

commit v5 on v4

--- a/solution.py
+++ b/solution.py
@@ -735,7 +735,7 @@
             first += tiles
         return carry
 
-    lax.fori_loop(0, 4, up, 0)
+    lax.fori_loop(0, 4, up, 0, unroll=2)
 
     mlp.last(mlp.down)
     mlp.last_to_mate(mlp.down)
@@ -761,7 +761,7 @@
         residual[...] += dot(hidden[y, :ROWS, :], down_weights(y, 0, 4), NT)
         return carry
 
-    lax.fori_loop(0, 4, down, 0)
+    lax.fori_loop(0, 4, down, 0, unroll=2)
     for n in range(4):
         pair_sends[2 + n].wait_recv()
     total = residual[...] + returned[...].astype(F32)

time: 101 us -> 101 us (level)
  no operation moved by 1% of the time
where the time goes in v5:
time: 101 us; the launch traced here: 100 us
  Pallas kernels  98.5 us (98%)
  local copies, waits for them, and re-layouts  1.78 us (2%)
    pallas_call x1, Pallas kernels, per_device(): pl.pallas_call(kernel, out_shape=jax.ShapeDtypeStruct((ROWS, D), BF), in_...  98.5 us

profile of v5, /device:TPU:1, one launch (start us, length us, event | category | flops | bytes accessed | tf_op | source)
XLA Modules:
  0.0 100.3 jit_solution(10483453042414666208)
XLA Ops:
  0.0 98.5 %layer.1 = bf16[160,1280]{1,0:T(8,128)(2,1)} custom-call(bf16[4,256,1280]{2,1,0:T(8,128)(2,1)} %patches.1, bf16[256,1280]{1,0:T(8,128)(2,1)} %position.1, s32[4,64]{1,0:T(4,128)} %keep.1, s32[512]{0:T(512)} %counts.1, s32[512]{0:T(512)} %offsets.1, f32[1,2,1280]{2,1,0:T(2,128)} %ln_gain.1, f32[1,2,1280]{2,1,0:T(2,128)} %ln_bias.1, ...), custom_call_target="tpu_custom_call" | custom-call | tf_op jit(solution)/shard_map/layer/pallas_call | solution.py:790
  98.5 1.8 %copy.17 = bf16[160,1280]{1,0:T(8,128)(2,1)} copy(bf16[160,1280]{1,0:T(8,128)(2,1)} %layer.1) | data formatting | bytes 819200
